TPU v7x, 32 devices: a whole 2x2x4 slice. The times are simulated.
32 devices in a mesh: train: 4 (over y, x), induce: 8 (over z, core).
Axes of the slice: x: 2, y: 2, z: 4, core: 2. Of those that a mesh axis runs over, the one named last changes fastest.
Arguments:
- train_coords: float32 [256, 192], P('train'), may hold values from -0.3 to 4.8, as said below
- induce_coords: float32 [1024, 192], P('induce'), may hold values from -0.3 to 4.8, as said below
- train_forces: float32 [256, 192], P('train'), may hold values from -18 to 18
- atom_pairs: int32 [2, 2016], replicated, may hold values from 0 to 63, as said below
- length_scale: float32 [1], replicated, may hold values from 1.5 to 3
Outputs:
- coefficients: float32 [1024, 192], P('induce')
- residual: float32 [1024, 192], P('induce')
- desc_coeffs: float32 [1024, 2016], P('induce')
Inputs may be any that keep to these rules, and one draw needn't show every extreme that they name: `atom_pairs`: every unordered pair of two different atoms of the 64 stands in exactly one column, in either order. `train_coords`: atom a lies within 0.3 of 1.5 * (a % 4, a // 4 % 4, a // 16) in each component. `induce_coords`: atom a lies within 0.3 of 1.5 * (a % 4, a // 4 % 4, a // 16) in each component.
All inputs are finite; a program needn't handle non-finite values.
Results may differ from a plain program's by a relative error of at most 0.0085.
Values sent between devices are 32-bit elements; how exact they have to be, the bound alone decides.
No kernel may reach another device: no remote copies, remote signals or barrier semaphores. Data moves between devices by JAX's collectives and lax.ppermute only.
A program may use at most 64 MiB of HBM per device.

v0:
```python
import math
import jax
import jax.numpy as jnp
from jax import lax
from jax.sharding import PartitionSpec as P

root_five = math.sqrt(5.0)


def make_incidence(atom_pairs, atom_count):
    atom_ids = jnp.arange(atom_count, dtype=jnp.int32)
    head_hit = (atom_pairs[0][:, None] == atom_ids[None, :]).astype(jnp.float32)
    tail_hit = (atom_pairs[1][:, None] == atom_ids[None, :]).astype(jnp.float32)
    return head_hit - tail_hit


def lattice_coords(atom_count):
    atom_ids = jnp.arange(atom_count, dtype=jnp.int32)
    lattice = jnp.stack([atom_ids % 4, atom_ids // 4 % 4, atom_ids // 16]).astype(jnp.float32)
    return (1.5 * lattice).reshape(1, 3 * atom_count)


def describe(coords, incidence):
    atom_count = incidence.shape[1]
    spatial = coords.reshape(coords.shape[0], 3, atom_count)
    offsets = jnp.einsum("bca,pa->bcp", spatial, incidence, precision=lax.Precision.HIGHEST)
    length = jnp.sqrt(jnp.sum(offsets * offsets, axis=1))
    return (1.0 / length, offsets / (length**3)[:, None, :])


def centered(coords, incidence):
    values, gradients = describe(coords, incidence)
    lattice_values = describe(lattice_coords(incidence.shape[1]), incidence)[0]
    return ((values - lattice_values).astype(jnp.bfloat16), gradients)


def to_desc(gradients, vectors, incidence):
    atom_count = incidence.shape[1]
    shifted = jnp.einsum(
        "bca,pa->bcp",
        vectors.reshape(vectors.shape[0], 3, atom_count),
        incidence,
        precision=lax.Precision.HIGHEST,
    )
    return -jnp.sum(gradients * shifted, axis=1)


def to_forces(gradients, values, incidence):
    weighted = gradients * values[:, None, :]
    summed = jnp.einsum("bcp,pa->bca", weighted, incidence, precision=lax.Precision.HIGHEST)
    return -summed.reshape(values.shape[0], -1)


def matern(row_desc, col_desc, length):
    inner_prod = jnp.dot(row_desc, col_desc.T, preferred_element_type=jnp.float32)
    row_sq = jnp.sum(jnp.square(row_desc.astype(jnp.float32)), axis=1)
    col_sq = jnp.sum(jnp.square(col_desc.astype(jnp.float32)), axis=1)
    radius = jnp.sqrt(row_sq[:, None] + col_sq[None, :] - 2.0 * inner_prod) / length
    falloff = jnp.exp(-root_five * radius)
    diag_part = 5.0 / (3.0 * length**2) * (1.0 + root_five * radius) * falloff
    outer_part = 25.0 / (3.0 * length**4) * falloff
    return (diag_part, outer_part)


def apply_forward(train_desc, induce_desc, diag_part, outer_part, induce_vals):
    self_dot = jnp.sum(induce_desc.astype(jnp.float32) * induce_vals.astype(jnp.float32), axis=1)
    projected = (
        jnp.dot(train_desc, induce_vals.T, preferred_element_type=jnp.float32) - self_dot[None, :]
    )
    product = outer_part * projected
    result = jnp.dot(
        diag_part.astype(jnp.bfloat16), induce_vals, preferred_element_type=jnp.float32
    )
    result = result + jnp.dot(
        product.astype(jnp.bfloat16), induce_desc, preferred_element_type=jnp.float32
    )
    return result - train_desc.astype(jnp.float32) * jnp.sum(product, axis=1)[:, None]


def apply_adjoint(train_desc, induce_desc, diag_part, outer_part, train_vals):
    self_dot = jnp.sum(train_desc.astype(jnp.float32) * train_vals.astype(jnp.float32), axis=1)
    projected = self_dot[:, None] - jnp.dot(
        train_vals, induce_desc.T, preferred_element_type=jnp.float32
    )
    product = outer_part * projected
    result = jnp.dot(
        diag_part.astype(jnp.bfloat16).T, train_vals, preferred_element_type=jnp.float32
    )
    result = result - jnp.dot(
        product.astype(jnp.bfloat16).T, train_desc, preferred_element_type=jnp.float32
    )
    return result + induce_desc.astype(jnp.float32) * jnp.sum(product, axis=0)[:, None]


def per_device(train_coords, induce_coords, train_forces, atom_pairs, length_scale):
    atom_count = train_coords.shape[1] // 3
    incidence = make_incidence(atom_pairs, atom_count)
    train_desc, train_grad = centered(train_coords, incidence)
    induce_desc, induce_grad = centered(induce_coords, incidence)
    diag_part, outer_part = matern(train_desc, induce_desc, length_scale[0])

    def forward(vectors):
        vectors = lax.all_gather(vectors, "train", axis=0, tiled=True)
        induce_vals = to_desc(induce_grad, vectors, incidence).astype(jnp.bfloat16)
        partial_forces = to_forces(
            train_grad,
            apply_forward(train_desc, induce_desc, diag_part, outer_part, induce_vals),
            incidence,
        )
        return lax.psum(partial_forces, "induce")

    def adjoint(forces_like):
        train_vals = to_desc(train_grad, forces_like, incidence).astype(jnp.bfloat16)
        partial_coeffs = to_forces(
            induce_grad,
            apply_adjoint(train_desc, induce_desc, diag_part, outer_part, train_vals),
            incidence,
        )
        return lax.psum_scatter(partial_coeffs, "train", scatter_dimension=0, tiled=True)

    start = adjoint(train_forces)
    probed = forward(start)
    probed_local = jnp.sum(probed * probed)
    cross_local = jnp.sum(train_forces * probed)
    probed_sq = lax.psum(probed_local, "train")
    cross_sq = lax.psum(cross_local, "train")
    quotient = probed_sq / cross_sq
    center = 0.775 * quotient
    spread = 0.725 * quotient
    momentum = spread / center
    direction = start / center
    coefficients = direction
    residual = start - adjoint(probed) / center
    momentum_next = 1.0 / (2.0 * center / spread - momentum)
    direction = momentum_next * momentum * direction + 2.0 * momentum_next / spread * residual
    coefficients = coefficients + direction
    residual = residual - adjoint(forward(direction))
    coefficients, residual = (
        lax.all_gather(coefficients, "train", axis=0, tiled=True),
        lax.all_gather(residual, "train", axis=0, tiled=True),
    )
    desc_coeffs = to_desc(induce_grad, coefficients, incidence)
    return (coefficients, residual, desc_coeffs)


def solution(mesh):
    in_specs = (P("train", None), P("induce", None), P("train", None), P(), P())
    out_specs = (P("induce", None), P("induce", None), P("induce", None))
    return jax.shard_map(
        per_device, mesh=mesh, in_specs=in_specs, out_specs=out_specs, check_vma=False
    )
```

profile of v0, /device:TPU:0, one launch (start us, length us, event | category | flops | bytes accessed | tf_op | source)
XLA Modules:
  0.0 235.9 jit_solution(11568177319664420499)
XLA Ops:
  12.8 4.5 %fusion = (f32[128,2016]{0,1:T(8,128)S(1)}, f32[2016,128,3]{1,0,2:T(8,128)}) fusion(f32[128,3,64]{0,2,1:T(8,128)S(1)} %bitcast.109, s32[2016]{0:T(1024)S(1)} %bitcast.136, s32[2016]{0:T(1024)S(1)} %bitcast.122), kind=kOutput, calls=%fused_computation.2 | convolution fusion | flops 596477952 | bytes 4243200 | tf_op jit(solution)/shard_map/bca,pa->bcp/dot_general | solution.py:26
  22.3 2.3 fusion.29
  25.4 27.0 %reduce-scatter.10.cloned.1.call-done = f32[32,192]{1,0:T(8,128)} async-done(((f32[128,192]{1,0:T(8,128)}), f32[32,192]{1,0:T(8,128)}) %reduce-scatter.10.cloned.1.call-update) | async-done | bytes 24592 | tf_op jit(solution)/shard_map/reduce_scatter | solution.py:119
  52.4 8.6 %all_gather.12 = f32[128,192]{1,0:T(8,128)S(1)} all-gather(f32[32,192]{1,0:T(8,128)} %reduce-scatter.10.cloned.1.call-done), channel_id=1, replica_groups=mesh['train'=4,'induce'=8] {'train'}, dimensions={0}, use_global_device_ids=true | all-gather | bytes 122880 | tf_op jit(solution)/shard_map/all_gather | solution.py:103
  61.1 5.3 %multiply_reduce_fusion.2 = f32[128,2016]{0,1:T(8,128)S(1)} fusion(f32[128,3,64]{0,2,1:T(8,128)S(1)} %bitcast.116, s32[2016]{0:T(1024)S(1)} %bitcast.139, s32[2016]{0:T(1024)S(1)} %bitcast.125, f32[128,2016]{0,1:T(8,128)S(1)} %get-tuple-element.20, f32[2016,128,3]{1,0,2:T(8,128)} %get-tuple-element.26), kind=kOutput, calls=%fused_computation.9 | convolution fusion | flops 597252096 | bytes 5275392 | tf_op jit(solution)/shard_map/bca,pa->bcp/dot_general | solution.py:39
  67.9 2.2 fusion.23
  71.7 28.0 %psum.28 = f32[64,192]{0,1:T(8,128)} all-reduce(f32[64,192]{0,1:T(8,128)} %bitcast.113), channel_id=1, replica_groups=mesh['train'=4,'induce'=8] {'induce'}, use_global_device_ids=true, to_apply=%region_12.13 | all-reduce | flops 12288 | bytes 98304 | tf_op jit(solution)/shard_map/psum | solution.py:110
  99.7 2.8 %fusion.21 = f32[64,2016]{1,0:T(8,128)S(1)} fusion(f32[64,3,64]{0,2,1:T(8,128)} %bitcast.112, s32[2016]{0:T(1024)S(1)} %bitcast.141, s32[2016]{0:T(1024)S(1)} %bitcast.127, f32[64,3,2016]{2,0,1:T(8,128)S(1)} %copy-done.5, f32[64,2016]{1,0:T(8,128)} %copy-done.6), kind=kOutput, calls=%fused_computation.44 | convolution fusion | flops 298948608 | bytes 2645760 | tf_op jit(solution)/shard_map/bca,pa->bcp/dot_general | solution.py:39
  104.4 2.9 %fusion.32 = f32[128,3,64]{0,2,1:T(8,128)} fusion(f32[128,2016]{0,1:T(8,128)S(1)} %fusion.9, s32[2016]{0:T(1024)S(1)} %bitcast.142, s32[2016]{0:T(1024)S(1)} %bitcast.128, f32[2016,128,3]{1,0,2:T(8,128)S(1)} %copy-done.2, f32[128,2016]{0,1:T(8,128)S(1)} %get-tuple-element.20), kind=kOutput, calls=%fused_computation.55 | convolution fusion | flops 596760576 | bytes 5275392 | tf_op jit(solution)/shard_map/bcp,pa->bca/dot_general | solution.py:50
  109.0 1.6 multiply_reduce_fusion.4
  110.7 9.5 %all-reduce = (f32[]{:T(128)}, f32[]{:T(128)}) all-reduce(f32[]{:T(128)} %get-tuple-element.12, f32[]{:T(128)} %get-tuple-element.11), channel_id=1, replica_groups=mesh['train'=4,'induce'=8] {'train'}, use_global_device_ids=true, to_apply=%region_14.15 | all-reduce | flops 2 | bytes 16 | tf_op jit(solution)/shard_map/psum | solution.py:125
  121.7 8.8 %reduce-scatter.12.cloned.1.call-done = f32[32,192]{1,0:T(8,128)} async-done(((f32[128,192]{1,0:T(8,128)}), f32[32,192]{1,0:T(8,128)}) %reduce-scatter.12.cloned.1.call-update) | async-done | bytes 24592 | tf_op jit(solution)/shard_map/reduce_scatter | solution.py:119
  131.9 9.3 %all_gather.14 = f32[128,192]{1,0:T(8,128)} all-gather(f32[32,192]{1,0:T(8,128)S(1)} %get-tuple-element.16), channel_id=1, replica_groups=mesh['train'=4,'induce'=8] {'train'}, dimensions={0}, use_global_device_ids=true | all-gather | bytes 122880 | tf_op jit(solution)/shard_map/all_gather | solution.py:103
  141.2 1.6 copy.45
  142.8 5.3 %multiply_reduce_fusion.1 = f32[128,2016]{0,1:T(8,128)S(1)} fusion(f32[128,3,64]{0,2,1:T(8,128)} %bitcast.118, s32[2016]{0:T(1024)S(1)} %bitcast.143, s32[2016]{0:T(1024)S(1)} %bitcast.129, f32[128,2016]{0,1:T(8,128)S(1)} %get-tuple-element.20, f32[2016,128,3]{1,0,2:T(8,128)} %get-tuple-element.26), kind=kOutput, calls=%fused_computation.6 | convolution fusion | flops 597252096 | bytes 5275392 | tf_op jit(solution)/shard_map/bca,pa->bcp/dot_general | solution.py:39
  149.5 2.2 fusion.26
  151.6 27.5 %psum.31 = f32[64,3,64]{2,0,1:T(8,128)S(1)} all-reduce(f32[64,3,64]{2,0,1:T(8,128)} %fusion.26), channel_id=1, replica_groups=mesh['train'=4,'induce'=8] {'induce'}, use_global_device_ids=true, to_apply=%region_24.25 | all-reduce | flops 12288 | bytes 98304 | tf_op jit(solution)/shard_map/psum | solution.py:110
  179.1 3.1 %fusion.22 = f32[64,2016]{1,0:T(8,128)S(1)} fusion(f32[64,3,64]{2,0,1:T(8,128)S(1)} %psum.31, s32[2016]{0:T(1024)S(1)} %bitcast.145, s32[2016]{0:T(1024)S(1)} %bitcast.131, f32[64,3,2016]{2,0,1:T(8,128)} %copy-done.4, f32[64,2016]{1,0:T(8,128)} %copy-done.6), kind=kOutput, calls=%fused_computation.45 | convolution fusion | flops 298948608 | bytes 2645760 | tf_op jit(solution)/shard_map/bca,pa->bcp/dot_general | solution.py:39
  182.8 8.5 %all_gather.13 = f32[128,192]{1,0:T(8,128)} all-gather(f32[32,192]{1,0:T(8,128)S(1)} %copy-done.11), channel_id=1, replica_groups=mesh['train'=4,'induce'=8] {'train'}, dimensions={0}, use_global_device_ids=true | all-gather | bytes 122880 | tf_op jit(solution)/shard_map/all_gather | solution.py:139
  191.2 1.6 copy.48
  194.8 2.3 fusion.35
  197.8 5.3 %multiply_reduce_fusion = f32[128,2016]{0,1:T(8,128)S(1)} fusion(f32[128,3,64]{0,2,1:T(8,128)S(1)} %bitcast.114, s32[2016]{0:T(1024)S(1)} %bitcast.147, s32[2016]{0:T(1024)S(1)} %bitcast.133, f32[128,2016]{0,1:T(8,128)S(1)} %get-tuple-element.20, f32[2016,128,3]{1,0,2:T(8,128)} %get-tuple-element.26), kind=kOutput, calls=%fused_computation.3 | convolution fusion | flops 597252096 | bytes 5275392 | tf_op jit(solution)/shard_map/bca,pa->bcp/dot_general | solution.py:39
  204.2 15.2 %reduce-scatter.14.cloned.1.call-done = f32[32,192]{1,0:T(8,128)} async-done(((f32[128,192]{1,0:T(8,128)}), f32[32,192]{1,0:T(8,128)}) %reduce-scatter.14.cloned.1.call-update) | async-done | bytes 24592 | tf_op jit(solution)/shard_map/reduce_scatter | solution.py:119
  220.1 8.5 %all_gather.15 = f32[128,192]{1,0:T(8,128)S(1)} all-gather(f32[32,192]{1,0:T(8,128)S(1)} %fusion.115), channel_id=1, replica_groups=mesh['train'=4,'induce'=8] {'train'}, dimensions={0}, use_global_device_ids=true | all-gather | bytes 122880 | tf_op jit(solution)/shard_map/all_gather | solution.py:140
  (75 shorter events, 25.8 us)
Async XLA Ops:
  7.2 5.7 %copy-start = (f32[128,192]{0,1:T(8,128)S(1)}, f32[128,192]{0,1:T(8,128)}, u32[]{:S(2)}) copy-start(f32[128,192]{0,1:T(8,128)} %param.6) | copy-start | bytes 294916
  7.2 45.2 %reduce-scatter.10.cloned.1.call-start = ((), (), s32[]{:S(2)}) async-start(), calls=%async_computation.3 | async-start | bytes 163840 | tf_op jit(solution)/shard_map/reduce_scatter | solution.py:119
  10.2 7.2 %copy-start.9 = (f32[64,192]{0,1:T(8,128)}, f32[64,192]{0,1:T(8,128)S(1)}, u32[]{:S(2)}) copy-start(f32[64,192]{0,1:T(8,128)S(1)} %copy.35) | copy-start | bytes 147460
  12.6 6.3 %copy-start.4 = (f32[64,3,2016]{2,0,1:T(8,128)}, f32[64,3,2016]{2,0,1:T(8,128)S(1)}, u32[]{:S(2)}) copy-start(f32[64,3,2016]{2,0,1:T(8,128)S(1)} %get-tuple-element.24) | copy-start | bytes 4644868
  12.8 6.2 %copy-start.6 = (f32[64,2016]{1,0:T(8,128)}, f32[64,2016]{1,0:T(8,128)S(1)}, u32[]{:S(2)}) copy-start(f32[64,2016]{1,0:T(8,128)S(1)} %multiply_multiply_fusion.1) | copy-start | bytes 1548292
  20.5 1.9 copy-start.1
  25.4 105.1 %reduce-scatter.12.cloned.1.call-start = ((), (), s32[]{:S(2)}) async-start(), calls=%async_computation.4 | async-start | bytes 163840 | tf_op jit(solution)/shard_map/reduce_scatter | solution.py:119
  66.4 1.4 copy-start.5
  66.4 1.5 copy-start.7
  102.5 1.9 copy-start.2
  109.0 110.4 %reduce-scatter.14.cloned.1.call-start = ((), (), s32[]{:S(2)}) async-start(), calls=%async_computation.5 | async-start | bytes 163840 | tf_op jit(solution)/shard_map/reduce_scatter | solution.py:119
  148.1 1.3 copy-start.8
  179.1 3.7 %copy-start.11 = (f32[32,192]{1,0:T(8,128)S(1)}, f32[32,192]{1,0:T(8,128)}, u32[]{:S(2)}) copy-start(f32[32,192]{1,0:T(8,128)} %get-tuple-element.15) | copy-start | bytes 73732
  192.9 1.9 copy-start.3
  194.7 3.0 %copy-start.13 = (f32[128,192]{0,1:T(8,128)S(1)}, f32[128,192]{0,1:T(8,128)}, u32[]{:S(2)}) copy-start(f32[128,192]{0,1:T(8,128)} %copy.48) | copy-start | bytes 294916
  197.8 21.5 %copy-start.10 = (f32[32,192]{1,0:T(8,128)S(1)}, f32[32,192]{1,0:T(8,128)}, u32[]{:S(2)}) copy-start(f32[32,192]{1,0:T(8,128)} %reduce-scatter.10.cloned.1.call-done) | copy-start | bytes 73732
  197.8 21.5 %copy-start.12 = (f32[32,192]{1,0:T(8,128)S(1)}, f32[32,192]{1,0:T(8,128)}, u32[]{:S(2)}) copy-start(f32[32,192]{1,0:T(8,128)} %reduce-scatter.12.cloned.1.call-done) | copy-start | bytes 73732
Sparse Core Ops, SparseCore 0:
  25.5 26.8 reduce-scatter.9
  109.1 21.3 reduce-scatter.11
  197.9 21.3 reduce-scatter.13
where the time goes:
time: 237 us; the launch traced here: 236 us
  blocking collectives  99.8 us (42%)
  waiting for transfers between devices  51 us (22%)
  matrix products  46.9 us (20%)
  between operations  16.3 us (7%)
  local copies, waits for them, and re-layouts  15 us (6%)
  other arithmetic  6.73 us (3%)
    psum x2, blocking collectives, forward(): return lax.psum(partial_forces, 'induce')  55.5 us
    reduce_scatter x3, waiting for transfers between devices, adjoint(): lax.psum_scatter(partial_coeffs, 'train', scatter_dimension=0, tiled=True)  51 us
    dot_general x6, matrix products, to_desc(): jnp.einsum('bca,pa->bcp', vectors.reshape(vectors.shape[0], 3, atom_count...  23.4 us
    all_gather x2, blocking collectives, forward(): vectors = lax.all_gather(vectors, 'train', axis=0, tiled=True)  17.8 us
    dot_general x5, matrix products, to_forces(): jnp.einsum('bcp,pa->bca', weighted, incidence, precision=lax.Precision.HI...  11.7 us
    unnamed x35, local copies, waits for them, and re-layouts  10.8 us
    psum x1, blocking collectives, per_device(): probed_sq = lax.psum(probed_local, 'train')  9.53 us
    all_gather x1, blocking collectives, per_device(): lax.all_gather(residual, 'train', axis=0, tiled=True)  8.46 us
  transfers between devices with their start and end apart: 3, of which 3 were waited for; matrix products, arithmetic and copies ran while one was open for 3% of the time, Pallas kernels for 0%

commit v1 on v0

--- a/solution.py
+++ b/solution.py
@@ -5,6 +5,12 @@
 from jax.sharding import PartitionSpec as P
 
 root_five = math.sqrt(5.0)
+
+
+def add_all(block, name):
+    pieces = lax.all_gather(block, name, axis=0, tiled=False)
+    summed = pieces.sum(axis=0)
+    return summed
 
 
 def make_incidence(atom_pairs, atom_count):
@@ -107,7 +113,7 @@
             apply_forward(train_desc, induce_desc, diag_part, outer_part, induce_vals),
             incidence,
         )
-        return lax.psum(partial_forces, "induce")
+        return add_all(partial_forces, "induce")
 
     def adjoint(forces_like):
         train_vals = to_desc(train_grad, forces_like, incidence).astype(jnp.bfloat16)

time: 237 us -> 217 us (0.916)
  blocking collectives: 99.8 us -> 74.2 us
  waiting for transfers between devices: 51 us -> 56.4 us
    psum x2 -> x0, blocking collectives: 55.5 us -> none  [forward(): return lax.psum(partial_forces, 'induce')]
    all_gather x0 -> x2, blocking collectives: none -> 29.9 us  [add_all(): pieces = lax.all_gather(block, name, axis=0, tiled=False)]
    reduce_scatter x3, waiting for transfers between devices: 51 us -> 56.3 us  [adjoint(): lax.psum_scatter(partial_coeffs, 'train', scatter_dimension=0, tiled=True)]
    unnamed x35 -> x39, local copies, waits for them, and re-layouts: 10.8 us -> 11.5 us
  transfers between devices with their start and end apart: 3 -> 3, of which waited for: 3 -> 3; matrix products, arithmetic and copies ran while one was open for 3% -> 4% of each run, Pallas kernels for 0% -> 0%
where the time goes in v1:
time: 217 us; the launch traced here: 216 us
  blocking collectives  74.2 us (34%)
  waiting for transfers between devices  56.4 us (26%)
  matrix products  46.4 us (21%)
  between operations  16.4 us (8%)
  local copies, waits for them, and re-layouts  15.5 us (7%)
  other arithmetic  6.73 us (3%)
    reduce_scatter x3, waiting for transfers between devices, adjoint(): lax.psum_scatter(partial_coeffs, 'train', scatter_dimension=0, tiled=True)  56.3 us
    all_gather x2, blocking collectives, add_all(): pieces = lax.all_gather(block, name, axis=0, tiled=False)  29.9 us
    dot_general x6, matrix products, to_desc(): jnp.einsum('bca,pa->bcp', vectors.reshape(vectors.shape[0], 3, atom_count...  23.4 us
    all_gather x2, blocking collectives, forward(): vectors = lax.all_gather(vectors, 'train', axis=0, tiled=True)  17.8 us
    unnamed x39, local copies, waits for them, and re-layouts  11.5 us
    dot_general x5, matrix products, to_forces(): jnp.einsum('bcp,pa->bca', weighted, incidence, precision=lax.Precision.HI...  11.2 us
    psum x1, blocking collectives, per_device(): probed_sq = lax.psum(probed_local, 'train')  9.53 us
    all_gather x1, blocking collectives, per_device(): lax.all_gather(residual, 'train', axis=0, tiled=True)  8.47 us
  transfers between devices with their start and end apart: 3, of which 3 were waited for; matrix products, arithmetic and copies ran while one was open for 4% of the time, Pallas kernels for 0%

profile of v1, /device:TPU:0, one launch (start us, length us, event | category | flops | bytes accessed | tf_op | source)
XLA Modules:
  0.0 215.7 jit_solution(9409854702809433740)
XLA Ops:
  12.8 4.5 %fusion = (f32[128,2016]{0,1:T(8,128)S(1)}, f32[2016,128,3]{1,0,2:T(8,128)}) fusion(f32[128,3,64]{0,2,1:T(8,128)S(1)} %bitcast.111, s32[2016]{0:T(1024)S(1)} %bitcast.140, s32[2016]{0:T(1024)S(1)} %bitcast.126), kind=kOutput, calls=%fused_computation.2 | convolution fusion | flops 596477952 | bytes 4243200 | tf_op jit(solution)/shard_map/bca,pa->bcp/dot_general | solution.py:32
  17.3 1.6 fusion.20
  22.3 2.3 %fusion.29 = f32[128,3,64]{0,2,1:T(8,128)S(1)} fusion(f32[128,2016]{0,1:T(8,128)S(1)} %fusion.10, s32[2016]{0:T(1024)S(1)} %bitcast.142, s32[2016]{0:T(1024)S(1)} %bitcast.128, f32[2016,128,3]{1,0,2:T(8,128)S(1)} %copy-done.1, f32[128,2016]{0,1:T(8,128)S(1)} %get-tuple-element.23), kind=kOutput, calls=%fused_computation.54 | convolution fusion | flops 596760576 | bytes 5275392 | tf_op jit(solution)/shard_map/bcp,pa->bca/dot_general | solution.py:56
  25.4 27.0 %reduce-scatter.10.cloned.1.call-done = f32[32,192]{1,0:T(8,128)} async-done(((f32[128,192]{1,0:T(8,128)}), f32[32,192]{1,0:T(8,128)}) %reduce-scatter.10.cloned.1.call-update) | async-done | bytes 24592 | tf_op jit(solution)/shard_map/reduce_scatter | solution.py:125
  52.5 8.6 %all_gather.20 = f32[128,192]{1,0:T(8,128)S(1)} all-gather(f32[32,192]{1,0:T(8,128)} %reduce-scatter.10.cloned.1.call-done), channel_id=1, replica_groups=mesh['train'=4,'induce'=8] {'train'}, dimensions={0}, use_global_device_ids=true | all-gather | bytes 122880 | tf_op jit(solution)/shard_map/all_gather | solution.py:109
  61.1 5.3 %multiply_reduce_fusion.2 = f32[128,2016]{0,1:T(8,128)S(1)} fusion(f32[128,3,64]{0,2,1:T(8,128)S(1)} %bitcast.117, s32[2016]{0:T(1024)S(1)} %bitcast.143, s32[2016]{0:T(1024)S(1)} %bitcast.129, f32[128,2016]{0,1:T(8,128)S(1)} %get-tuple-element.23, f32[2016,128,3]{1,0,2:T(8,128)} %get-tuple-element.29), kind=kOutput, calls=%fused_computation.9 | convolution fusion | flops 597252096 | bytes 5275392 | tf_op jit(solution)/shard_map/bca,pa->bcp/dot_general | solution.py:45
  69.7 15.0 %all_gather.21 = f32[8,64,192]{2,1,0:T(8,128)S(1)} all-gather(f32[1,64,192]{2,1,0:T(8,128)S(1)} %copy.68), channel_id=1, replica_groups=mesh['train'=4,'induce'=8] {'induce'}, dimensions={0}, use_global_device_ids=true | all-gather | bytes 442368 | tf_op jit(solution)/shard_map/all_gather | solution.py:11
  85.3 2.7 %fusion.21 = f32[64,2016]{1,0:T(8,128)S(1)} fusion(f32[64,3,64]{0,2,1:T(8,128)S(1)} %bitcast.123, s32[2016]{0:T(1024)S(1)} %bitcast.145, s32[2016]{0:T(1024)S(1)} %bitcast.131, f32[64,3,2016]{2,0,1:T(8,128)S(1)} %copy-done.5, f32[64,2016]{1,0:T(8,128)} %copy-done.9), kind=kOutput, calls=%fused_computation.44 | convolution fusion | flops 298948608 | bytes 2645760 | tf_op jit(solution)/shard_map/bca,pa->bcp/dot_general | solution.py:45
  90.2 2.9 %fusion.32 = f32[128,3,64]{0,2,1:T(8,128)} fusion(f32[128,2016]{0,1:T(8,128)S(1)} %fusion.9, s32[2016]{0:T(1024)S(1)} %bitcast.146, s32[2016]{0:T(1024)S(1)} %bitcast.132, f32[2016,128,3]{1,0,2:T(8,128)S(1)} %copy-done.2, f32[128,2016]{0,1:T(8,128)S(1)} %copy-done.7), kind=kOutput, calls=%fused_computation.55 | convolution fusion | flops 596760576 | bytes 5275392 | tf_op jit(solution)/shard_map/bcp,pa->bca/dot_general | solution.py:56
  93.1 1.6 copy.89
  96.4 9.5 %all-reduce = (f32[]{:T(128)}, f32[]{:T(128)}) all-reduce(f32[]{:T(128)} %get-tuple-element.15, f32[]{:T(128)} %get-tuple-element.14), channel_id=1, replica_groups=mesh['train'=4,'induce'=8] {'train'}, use_global_device_ids=true, to_apply=%region_14.15 | all-reduce | flops 2 | bytes 16 | tf_op jit(solution)/shard_map/psum | solution.py:131
  107.5 11.5 %reduce-scatter.12.cloned.1.call-done = f32[32,192]{1,0:T(8,128)} async-done(((f32[128,192]{1,0:T(8,128)}), f32[32,192]{1,0:T(8,128)}) %reduce-scatter.12.cloned.1.call-update) | async-done | bytes 24592 | tf_op jit(solution)/shard_map/reduce_scatter | solution.py:125
  120.4 9.3 %all_gather.23 = f32[128,192]{1,0:T(8,128)} all-gather(f32[32,192]{1,0:T(8,128)S(1)} %get-tuple-element.19), channel_id=1, replica_groups=mesh['train'=4,'induce'=8] {'train'}, dimensions={0}, use_global_device_ids=true | all-gather | bytes 122880 | tf_op jit(solution)/shard_map/all_gather | solution.py:109
  129.6 1.6 copy.74
  131.3 5.3 %multiply_reduce_fusion.1 = f32[128,2016]{0,1:T(8,128)S(1)} fusion(f32[128,3,64]{0,2,1:T(8,128)} %bitcast.119, s32[2016]{0:T(1024)S(1)} %bitcast.147, s32[2016]{0:T(1024)S(1)} %bitcast.133, f32[128,2016]{0,1:T(8,128)S(1)} %copy-done.7, f32[2016,128,3]{1,0,2:T(8,128)} %get-tuple-element.29), kind=kOutput, calls=%fused_computation.6 | convolution fusion | flops 597252096 | bytes 5275392 | tf_op jit(solution)/shard_map/bca,pa->bcp/dot_general | solution.py:45
  137.9 2.2 %fusion.26 = f32[64,3,64]{2,0,1:T(8,128)} fusion(f32[64,2016]{1,0:T(8,128)S(1)} %fusion.11, s32[2016]{0:T(1024)S(1)} %bitcast.148, s32[2016]{0:T(1024)S(1)} %bitcast.134, f32[64,3,2016]{2,0,1:T(8,128)S(1)} %copy-done.5, f32[64,2016]{1,0:T(8,128)S(1)} %copy-done.11), kind=kOutput, calls=%fused_computation.53 | convolution fusion | flops 298702848 | bytes 2645760 | tf_op jit(solution)/shard_map/bcp,pa->bca/dot_general | solution.py:56
  141.2 15.0 %all_gather.24 = f32[8,64,192]{2,1,0:T(8,128)S(1)} all-gather(f32[1,64,192]{2,1,0:T(8,128)S(1)} %copy.76), channel_id=1, replica_groups=mesh['train'=4,'induce'=8] {'induce'}, dimensions={0}, use_global_device_ids=true | all-gather | bytes 442368 | tf_op jit(solution)/shard_map/all_gather | solution.py:11
  156.3 3.1 %fusion.22 = f32[64,2016]{1,0:T(8,128)S(1)} fusion(f32[64,3,64]{0,2,1:T(8,128)S(1)} %bitcast.122, s32[2016]{0:T(1024)S(1)} %bitcast.149, s32[2016]{0:T(1024)S(1)} %bitcast.135, f32[64,3,2016]{2,0,1:T(8,128)} %copy-done.4, f32[64,2016]{1,0:T(8,128)} %copy-done.9), kind=kOutput, calls=%fused_computation.45 | convolution fusion | flops 298948608 | bytes 2645760 | tf_op jit(solution)/shard_map/bca,pa->bcp/dot_general | solution.py:45
  160.0 8.4 %all_gather.22 = f32[128,192]{1,0:T(8,128)} all-gather(f32[32,192]{1,0:T(8,128)S(1)} %copy-done.13), channel_id=1, replica_groups=mesh['train'=4,'induce'=8] {'train'}, dimensions={0}, use_global_device_ids=true | all-gather | bytes 122880 | tf_op jit(solution)/shard_map/all_gather | solution.py:145
  168.4 1.6 copy.81
  172.0 2.3 %fusion.35 = f32[128,3,64]{0,2,1:T(8,128)S(1)} fusion(f32[128,2016]{0,1:T(8,128)S(1)} %fusion.8, s32[2016]{0:T(1024)S(1)} %bitcast.150, s32[2016]{0:T(1024)S(1)} %bitcast.136, f32[2016,128,3]{1,0,2:T(8,128)S(1)} %copy-done.3, f32[128,2016]{0,1:T(8,128)S(1)} %copy-done.7), kind=kOutput, calls=%fused_computation.56 | convolution fusion | flops 596760576 | bytes 5275392 | tf_op jit(solution)/shard_map/bcp,pa->bca/dot_general | solution.py:56
  175.1 5.3 %multiply_reduce_fusion = f32[128,2016]{0,1:T(8,128)S(1)} fusion(f32[128,3,64]{0,2,1:T(8,128)S(1)} %bitcast.115, s32[2016]{0:T(1024)S(1)} %bitcast.151, s32[2016]{0:T(1024)S(1)} %bitcast.137, f32[128,2016]{0,1:T(8,128)S(1)} %copy-done.7, f32[2016,128,3]{1,0,2:T(8,128)} %get-tuple-element.29), kind=kOutput, calls=%fused_computation.3 | convolution fusion | flops 597252096 | bytes 5275392 | tf_op jit(solution)/shard_map/bca,pa->bcp/dot_general | solution.py:45
  181.4 17.8 %reduce-scatter.14.cloned.1.call-done = f32[32,192]{1,0:T(8,128)} async-done(((f32[128,192]{1,0:T(8,128)}), f32[32,192]{1,0:T(8,128)}) %reduce-scatter.14.cloned.1.call-update) | async-done | bytes 24592 | tf_op jit(solution)/shard_map/reduce_scatter | solution.py:125
  200.0 8.5 %all_gather.25 = f32[128,192]{1,0:T(8,128)S(1)} all-gather(f32[32,192]{1,0:T(8,128)S(1)} %fusion.115), channel_id=1, replica_groups=mesh['train'=4,'induce'=8] {'train'}, dimensions={0}, use_global_device_ids=true | all-gather | bytes 122880 | tf_op jit(solution)/shard_map/all_gather | solution.py:146
  (86 shorter events, 26.3 us)
Async XLA Ops:
  7.2 5.6 %copy-start = (f32[128,192]{0,1:T(8,128)S(1)}, f32[128,192]{0,1:T(8,128)}, u32[]{:S(2)}) copy-start(f32[128,192]{0,1:T(8,128)} %param.6) | copy-start | bytes 294916
  7.2 45.3 %reduce-scatter.10.cloned.1.call-start = ((), (), s32[]{:S(2)}) async-start(), calls=%async_computation.3 | async-start | bytes 163840 | tf_op jit(solution)/shard_map/reduce_scatter | solution.py:125
  12.6 6.4 %copy-start.4 = (f32[64,3,2016]{2,0,1:T(8,128)}, f32[64,3,2016]{2,0,1:T(8,128)S(1)}, u32[]{:S(2)}) copy-start(f32[64,3,2016]{2,0,1:T(8,128)S(1)} %get-tuple-element.27) | copy-start | bytes 4644868
  12.8 6.2 %copy-start.9 = (f32[64,2016]{1,0:T(8,128)}, f32[64,2016]{1,0:T(8,128)S(1)}, u32[]{:S(2)}) copy-start(f32[64,2016]{1,0:T(8,128)S(1)} %multiply_multiply_fusion.1) | copy-start | bytes 1548292
  19.7 41.4 %copy-start.6 = (f32[128,2016]{0,1:T(8,128)}, f32[128,2016]{0,1:T(8,128)S(1)}, u32[]{:S(2)}) copy-start(f32[128,2016]{0,1:T(8,128)S(1)} %get-tuple-element.23) | copy-start | bytes 3096580
  20.4 1.9 copy-start.1
  25.4 93.6 %reduce-scatter.12.cloned.1.call-start = ((), (), s32[]{:S(2)}) async-start(), calls=%async_computation.4 | async-start | bytes 163840 | tf_op jit(solution)/shard_map/reduce_scatter | solution.py:125
  66.4 1.4 copy-start.5
  66.4 1.5 copy-start.10
  84.7 0.6 copy-start.8
  88.1 1.9 copy-start.2
  88.1 2.1 copy-start.7
  94.8 104.4 %reduce-scatter.14.cloned.1.call-start = ((), (), s32[]{:S(2)}) async-start(), calls=%async_computation.5 | async-start | bytes 163840 | tf_op jit(solution)/shard_map/reduce_scatter | solution.py:125
  136.6 1.3 copy-start.11
  156.3 3.7 %copy-start.13 = (f32[32,192]{1,0:T(8,128)S(1)}, f32[32,192]{1,0:T(8,128)}, u32[]{:S(2)}) copy-start(f32[32,192]{1,0:T(8,128)} %get-tuple-element.18) | copy-start | bytes 73732
  170.1 1.9 copy-start.3
  172.0 3.1 %copy-start.15 = (f32[128,192]{0,1:T(8,128)S(1)}, f32[128,192]{0,1:T(8,128)}, u32[]{:S(2)}) copy-start(f32[128,192]{0,1:T(8,128)} %copy.81) | copy-start | bytes 294916
  175.0 24.2 %copy-start.12 = (f32[32,192]{1,0:T(8,128)S(1)}, f32[32,192]{1,0:T(8,128)}, u32[]{:S(2)}) copy-start(f32[32,192]{1,0:T(8,128)} %reduce-scatter.10.cloned.1.call-done) | copy-start | bytes 73732
  175.0 24.2 %copy-start.14 = (f32[32,192]{1,0:T(8,128)S(1)}, f32[32,192]{1,0:T(8,128)}, u32[]{:S(2)}) copy-start(f32[32,192]{1,0:T(8,128)} %reduce-scatter.12.cloned.1.call-done) | copy-start | bytes 73732
Sparse Core Ops, SparseCore 0:
  25.5 26.8 reduce-scatter.9
  94.9 24.0 reduce-scatter.11
  175.1 24.0 reduce-scatter.13
